TPU v7x, 128 devices: a whole 4x4x4 slice. The times are simulated.
128 devices in a mesh: node: 128 (over z, x, y, core).
Axes of the slice: x: 4, y: 4, z: 4, core: 2. Of those that a mesh axis runs over, the one named last changes fastest.
Arguments:
- labels: bfloat16 [524288, 512], P('node'), may hold values from -6 to 6
- seed_mask: int32 [524288], P('node'), may hold values 0 or 1
- band_w: bfloat16 [4096, 3, 128, 128], P('node'), may hold values from 0.0009994507 to 1
- far_block: int32 [128, 128, 2], P('node'), may hold values from 0 to 511
- far_tile: int32 [128, 128, 2], P('node'), may hold values from 0 to 31
- far_count: int32 [128, 128], P('node'), may hold values from 0 to 2, as said below
- far_w: bfloat16 [128, 128, 2, 8, 128], P('node'), may hold values from 0.049804688 to 2
Outputs:
- final_labels: bfloat16 [524288, 512], P('node')
- residual: float32 [2, 4096], P(None, 'node')
Inputs may be any that keep to these rules, and one draw needn't show every extreme that they name: `far_count`: in every draw at least one destination shard has all 2 slots live from every source shard; other counts vary from pair to pair.
All inputs are finite; a program needn't handle non-finite values. No bound on the sum of `seed_mask` on one device may be relied on, other than what follows from the above.
Results may differ from a plain program's by a relative error of at most 0.0027.
Values may be sent and summed in bfloat16 or wider, within the bound.
A program may use at most 128 MiB of HBM per device.

v0:
```python
import jax
import jax.numpy as jnp
from jax import lax
from jax.sharding import PartitionSpec as P

ITERS = 2


def with_halo(block, sides, width):
    for axis, dim in sides:
        count = lax.axis_size(axis)
        forward = [(i, i + 1) for i in range(count - 1)]
        forward.append((count - 1, 0))
        backward = [(target, source) for source, target in forward]
        low = lax.ppermute(
            lax.slice_in_dim(block, block.shape[dim] - width, None, axis=dim), axis, forward
        )
        high = lax.ppermute(lax.slice_in_dim(block, 0, width, axis=dim), axis, backward)
        block = jnp.concatenate([low, block, high], axis=dim)
    return block


def fetch_blocks(current, requests, block_rows, classes):
    blocks = current.reshape(-1, block_rows, classes)[requests]
    return lax.all_to_all(blocks, "node", split_axis=0, concat_axis=0, tiled=True)


def cycle_tiles(current, tile_count, tile_rows, classes):
    tiles = current.reshape(tile_count, tile_rows, classes)
    return with_halo(tiles, (("node", 0),), 1)


def body(labels, seed_mask, band_w, far_block, far_tile, far_count, far_w):
    node_rows, classes = labels.shape
    tile_count = band_w.shape[0]
    tile_rows = band_w.shape[2]
    peer_count = far_w.shape[1]
    slot_count = far_w.shape[2]
    block_rows = far_w.shape[3]
    requests = lax.all_to_all(far_block, "node", split_axis=1, concat_axis=0, tiled=True).reshape(
        peer_count, slot_count
    )
    live_slots = jnp.arange(slot_count)[None, :] < far_count[0][:, None]
    weights = jnp.where(live_slots[:, :, None, None], far_w[0], jnp.zeros((), jnp.bfloat16))
    flat_tiles = far_tile[0].reshape(-1)
    weight_sums = jnp.sum(weights, axis=2, dtype=jnp.float32).reshape(-1, tile_rows)
    degree_far = jnp.zeros((tile_count, tile_rows), jnp.float32).at[flat_tiles].add(weight_sums)
    degree = jnp.sum(band_w, axis=(1, 3), dtype=jnp.float32) + degree_far
    slot_weights = weights.reshape(peer_count * slot_count, block_rows, tile_rows)
    onehot = jnp.arange(tile_count)[:, None] == flat_tiles[None, :]
    placed = jnp.where(onehot[:, :, None, None], slot_weights[None], jnp.zeros((), jnp.bfloat16))
    placed = placed.reshape(tile_count, peer_count * slot_count * block_rows, tile_rows)
    seeded = (seed_mask == 1).reshape(tile_count, tile_rows, 1)
    clamped = labels.astype(jnp.float32).reshape(tile_count, tile_rows, classes)
    current = labels
    residuals = []
    for sweep in range(ITERS):
        padded = cycle_tiles(current, tile_count, tile_rows, classes)
        received = fetch_blocks(current, requests, block_rows, classes)
        band_sum = jnp.zeros((tile_count, tile_rows, classes), jnp.float32)
        for offset in (-1, 0, 1):
            source = padded[1 + offset : 1 + offset + tile_count]
            band_sum = band_sum + jnp.einsum(
                "itr,irc->itc", band_w[:, offset + 1], source, preferred_element_type=jnp.float32
            )
        far_sum = jnp.einsum(
            "tqr,qc->trc", placed, received.reshape(-1, classes), preferred_element_type=jnp.float32
        )
        averaged = (band_sum + far_sum) / degree[:, :, None]
        row_scale = jnp.sqrt(jnp.mean(averaged * averaged, axis=2, keepdims=True))
        scaled = averaged / jnp.maximum(row_scale, 0.05)
        fresh = jnp.where(seeded, clamped, scaled).astype(jnp.bfloat16)
        previous = current.astype(jnp.float32).reshape(tile_count, tile_rows, classes)
        residuals.append(jnp.sum(jnp.abs(fresh.astype(jnp.float32) - previous), axis=(1, 2)))
        current = fresh.reshape(node_rows, classes)
    return (current, jnp.stack(residuals))


def solution(mesh):
    placed = (
        P("node", None),
        P("node"),
        P("node", None, None, None),
        P("node", None, None),
        P("node", None, None),
        P("node", None),
        P("node", None, None, None, None),
    )
    return jax.shard_map(
        body,
        mesh=mesh,
        in_specs=placed,
        out_specs=(P("node", None), P(None, "node")),
        check_vma=False,
    )
```

profile of v0, /device:TPU:0, one launch (start us, length us, event | category | flops | bytes accessed | tf_op | source)
XLA Modules:
  0.0 184.5 jit_solution(16199250453833278590)
XLA Ops:
  0.6 1.4 copy.27
  2.0 11.2 %all-to-all-start = ((s32[1,128,2]{2,0,1:T(1,128)}), s32[1,128,2]{2,0,1:T(1,128)S(1)}, u32[]{:S(2)}, u32[]{:S(2)}) async-start(s32[1,128,2]{2,0,1:T(1,128)} %copy.27), calls=%async_computation | async-start | bytes 131072 | tf_op jit(solution)/shard_map/all_to_all | solution.py:40
  13.2 1.0 slice_bitcast_fusion
  14.2 7.1 %collective-permute-start.1 = (bf16[1,128,512]{2,1,0:T(8,128)(2,1)S(1)}, bf16[1,128,512]{2,1,0:T(8,128)(2,1)S(1)}, u32[]{:S(2)}, u32[]{:S(2)}) collective-permute-start(bf16[1,128,512]{2,1,0:T(8,128)(2,1)S(1)} %get-tuple-element.6), channel_id=1, source_target_pairs={{1,0},{2,1},{3,2},{4,3},{5,4},{6,5},{7,6},{8,7},{9,8},{10,9},{11,1... | collective-permute-start | bytes 393224 | tf_op jit(solution)/shard_map/ppermute | solution.py:18
  21.3 0.7 iota_compare_fusion.1
  22.1 0.1 lt.51
  22.2 0.1 broadcast_in_dim.74
  22.3 0.1 broadcast_in_dim.75
  22.4 0.8 copy.24
  23.2 0.1 eq.28
  23.4 1.4 bitcast_select_fusion.1
  24.8 0.1 iota_compare_fusion
  24.9 0.1 reshape.183
  25.0 0.0 copy-start.6
  25.1 4.3 %gather_fusion = bf16[256,8,512]{2,1,0:T(8,128)(2,1)} fusion(bf16[512,8,512]{2,1,0:T(8,128)(2,1)} %bitcast.75, s32[1024]{0:T(1024)S(1)} %pad_clamp_fusion), kind=kCustom, calls=%fused_computation | custom fusion | bytes 4195328 | tf_op jit(solution)/shard_map/gather | solution.py:24
  29.4 9.6 %all-to-all-start.1 = ((bf16[128,2,8,512]{3,2,1,0:T(8,128)(2,1)}), bf16[128,2,8,512]{3,2,1,0:T(8,128)(2,1)}, u32[]{:S(2)}, u32[]{:S(2)}) async-start(bf16[128,2,8,512]{3,2,1,0:T(8,128)(2,1)} %bitcast.14), calls=%async_computation.1 | async-start | bytes 4194304 | tf_op jit(solution)/shard_map/all_to_all | solution.py:25
  39.0 0.1 broadcast_bitcast_fusion
  39.1 0.1 reshape_squeeze.3
  39.3 0.3 copy.25
  39.6 0.2 copy.26
  39.9 0.5 convert_reduce_fusion.1
  40.4 2.5 %convert_reduce_fusion = f32[32,128]{1,0:T(8,128)S(1)} fusion(bf16[32,3,128,128]{3,2,1,0:T(8,128)(2,1)} %param.9), kind=kLoop, calls=%fused_computation.29 | loop fusion | flops 3141632 | bytes 3162112 | tf_op jit(solution)/shard_map/reduce_sum | solution.py:48
  42.9 2.1 %scatter_fusion = f32[32,128]{1,0:T(8,128)S(1)} fusion(f32[32,128]{1,0:T(8,128)S(1)} %convert_reduce_fusion, s32[256]{0:T(256)S(1)} %bitcast.85, f32[256,128]{1,0:T(8,128)S(1)} %bitcast.83), kind=kCustom, calls=%fused_computation.2 | custom fusion | flops 32768 | bytes 394240 | tf_op jit(solution)/shard_map/scatter-add | solution.py:47
  45.0 0.0 copy-start.7
  45.0 0.0 copy-start
  45.1 7.1 %fusion.29 = f32[32,128,512]{2,1,0:T(8,128)} fusion(bf16[32,128,512]{2,1,0:T(8,128)(2,1)} %bitcast.76, bf16[32,3,128,128]{3,2,1,0:T(8,128)(2,1)} %param.9), kind=kOutput, calls=%fused_computation.46 | convolution fusion | flops 536870912 | bytes 13631488 | tf_op jit(solution)/shard_map/itr,irc->itc/dot_general | solution.py:63
  52.2 0.0 collective-permute-done
  52.2 5.7 %fusion.23 = f32[32,512,128]{1,2,0:T(8,128)} fusion(bf16[32,128,512]{2,1,0:T(8,128)(2,1)S(1)} %bitcast.77, bf16[1,128,512]{2,1,0:T(8,128)(2,1)S(1)} %collective-permute-done, bf16[32,3,128,128]{3,2,1,0:T(8,128)(2,1)} %param.9), kind=kOutput, calls=%fused_computation.40 | convolution fusion | flops 545259520 | bytes 13762560 | tf_op jit(solution)/shard_map/itr,irc->itc/dot_general | solution.py:63
  57.9 11.0 %all-to-all-done.1 = bf16[128,2,8,512]{3,2,1,0:T(8,128)(2,1)} async-done(((bf16[128,2,8,512]{3,2,1,0:T(8,128)(2,1)}), bf16[128,2,8,512]{3,2,1,0:T(8,128)(2,1)}, u32[]{:S(2)}, u32[]{:S(2)}) %all-to-all-start.1) | async-done | bytes 2097184 | tf_op jit(solution)/shard_map/all_to_all | solution.py:25
  68.9 12.9 %fusion.2 = f32[32,128,512]{2,1,0:T(8,128)} fusion(bf16[2048,512,1]{1,0,2:T(8,128)(2,1)} %bitcast.16, pred[32,2048]{1,0:T(8,128)(4,1)S(1)} %copy.25, bf16[2048,128]{0,1:T(8,128)(2,1)S(1)} %copy.26), kind=kOutput, calls=%fused_computation.5 | convolution fusion | flops 8598323200 | bytes 11075584 | tf_op jit(solution)/shard_map/tqr,qc->trc/dot_general | solution.py:66
  81.8 0.0 collective-permute-done.1
  81.8 13.5 %multiply_reduce_fusion.1 = (f32[32,128]{1,0:T(8,128)S(1)}, f32[32,128,512]{2,1,0:T(8,128)}) fusion(f32[32,128]{1,0:T(8,128)S(1)} %scatter_fusion, f32[32,128,512]{2,1,0:T(8,128)} %fusion.2, bf16[1,128,512]{2,1,0:T(8,128)(2,1)S(1)} %collective-permute-done.1, bf16[32,128,512]{2,1,0:T(8,128)(2,1)S(1)} %bitcast.78, bf16[32,3,128,128]{3,2,1,0:T(8,128)(2,1)} %param.9, ...), kind=kOutput, calls=%fused_computation.24 | convolution fusion | flops 557838336 | bytes 38961152 | tf_op jit(solution)/shard_map/itr,irc->itc/dot_general | solution.py:63
  95.4 7.1 %fusion.8 = bf16[32,128,512]{2,1,0:T(8,128)(2,1)} fusion(f32[32,128,512]{2,1,0:T(8,128)} %get-tuple-element.9, f32[32,128]{1,0:T(8,128)S(1)} %maximum_multiply_fusion.1, pred[32,128]{1,0:T(8,128)(4,1)S(1)} %compare_bitcast_fusion, bf16[4096,512]{1,0:T(8,128)(2,1)S(1)} %copy-done.1), kind=kLoop, calls=%fused_computation.15 | loop fusion | flops 8388608 | bytes 16797696 | tf_op jit(solution)/shard_map/convert_element_type | solution.py:72
  102.5 4.3 %gather_fusion.1 = bf16[256,8,512]{2,1,0:T(8,128)(2,1)} fusion(bf16[512,8,512]{2,1,0:T(8,128)(2,1)} %bitcast.80, s32[1024]{0:T(1024)S(1)} %pad_clamp_fusion), kind=kCustom, calls=%fused_computation.1 | custom fusion | bytes 4195328 | tf_op jit(solution)/shard_map/gather | solution.py:24
  106.8 5.8 %all-to-all-start.2 = ((bf16[128,2,8,512]{3,2,1,0:T(8,128)(2,1)}), bf16[128,2,8,512]{3,2,1,0:T(8,128)(2,1)}, u32[]{:S(2)}, u32[]{:S(2)}) async-start(bf16[128,2,8,512]{3,2,1,0:T(8,128)(2,1)} %bitcast.82), calls=%async_computation.2 | async-start | bytes 4194304 | tf_op jit(solution)/shard_map/all_to_all | solution.py:25
  112.6 1.0 fusion.45
  113.6 0.0 copy-start.3
  113.6 0.1 collective-permute-start.2
  113.7 7.1 %fusion.27 = f32[32,512,128]{1,2,0:T(8,128)} fusion(bf16[32,128,512]{2,1,0:T(8,128)(2,1)} %fusion.8, bf16[32,3,128,128]{3,2,1,0:T(8,128)(2,1)} %param.9), kind=kOutput, calls=%fused_computation.44 | convolution fusion | flops 536870912 | bytes 13631488 | tf_op jit(solution)/shard_map/itr,irc->itc/dot_general | solution.py:63
  120.8 7.2 %collective-permute-start.3 = (bf16[1,128,512]{2,1,0:T(8,128)(2,1)S(1)}, bf16[1,128,512]{2,1,0:T(8,128)(2,1)S(1)}, u32[]{:S(2)}, u32[]{:S(2)}) collective-permute-start(bf16[1,128,512]{2,1,0:T(8,128)(2,1)S(1)} %get-tuple-element.4), channel_id=1, source_target_pairs={{1,0},{2,1},{3,2},{4,3},{5,4},{6,5},{7,6},{8,7},{9,8},{10,9},{11,1... | collective-permute-start | bytes 393224 | tf_op jit(solution)/shard_map/ppermute | solution.py:18
  127.9 15.6 %collective-permute-done.2 = bf16[1,128,512]{2,1,0:T(8,128)(2,1)S(1)} collective-permute-done((bf16[1,128,512]{2,1,0:T(8,128)(2,1)S(1)}, bf16[1,128,512]{2,1,0:T(8,128)(2,1)S(1)}, u32[]{:S(2)}, u32[]{:S(2)}) %collective-permute-start.2) | collective-permute-done | bytes 131104 | tf_op jit(solution)/shard_map/ppermute | solution.py:15
  143.6 5.7 %fusion.19 = f32[32,512,128]{1,2,0:T(8,128)} fusion(bf16[32,128,512]{2,1,0:T(8,128)(2,1)S(1)} %copy-done.3, bf16[1,128,512]{2,1,0:T(8,128)(2,1)S(1)} %collective-permute-done.2, bf16[32,3,128,128]{3,2,1,0:T(8,128)(2,1)} %param.9), kind=kOutput, calls=%fused_computation.34 | convolution fusion | flops 545259520 | bytes 13762560 | tf_op jit(solution)/shard_map/itr,irc->itc/dot_general | solution.py:63
  149.3 12.9 %fusion = f32[32,128,512]{2,1,0:T(8,128)} fusion(bf16[2048,512,1]{1,0,2:T(8,128)(2,1)} %bitcast.24, pred[32,2048]{1,0:T(8,128)(4,1)S(1)} %copy.25, bf16[2048,128]{0,1:T(8,128)(2,1)S(1)} %copy.26), kind=kOutput, calls=%fused_computation.3 | convolution fusion | flops 8598323200 | bytes 11075584 | tf_op jit(solution)/shard_map/tqr,qc->trc/dot_general | solution.py:66
  162.2 13.7 %multiply_reduce_fusion = (f32[32,128]{1,0:T(8,128)S(1)}, f32[32,128,512]{2,1,0:T(8,128)}) fusion(f32[32,128]{1,0:T(8,128)S(1)} %scatter_fusion, f32[32,128,512]{2,1,0:T(8,128)} %fusion, bf16[1,128,512]{2,1,0:T(8,128)(2,1)S(1)} %collective-permute-done.3, bf16[32,128,512]{2,1,0:T(8,128)(2,1)S(1)} %copy-done.4, bf16[32,3,128,128]{3,2,1,0:T(8,128)(2,1)} %param.9, ...), kind=kOutput, calls=%fused_computation.23 | convolution fusion | flops 557838336 | bytes 38961152 | tf_op jit(solution)/shard_map/itr,irc->itc/dot_general | solution.py:63
  175.9 5.0 %fusion.9 = bf16[32,128,512]{2,1,0:T(8,128)(2,1)S(1)} fusion(f32[32,128,512]{2,1,0:T(8,128)} %get-tuple-element.11, f32[32,128]{1,0:T(8,128)S(1)} %maximum_multiply_fusion, pred[32,128]{1,0:T(8,128)(4,1)S(1)} %compare_bitcast_fusion, bf16[4096,512]{1,0:T(8,128)(2,1)S(1)} %copy-done.2), kind=kLoop, calls=%fused_computation.16 | loop fusion | flops 8388608 | bytes 16797696 | tf_op jit(solution)/shard_map/convert_element_type | solution.py:72
  180.9 0.0 copy-start.5
  180.9 3.1 %fusion.11 = (f32[32]{0:T(128)S(1)}, f32[32]{0:T(128)S(1)}) fusion(bf16[32,128,512]{2,1,0:T(8,128)(2,1)S(1)} %bitcast.79, bf16[32,128,512]{2,1,0:T(8,128)(2,1)S(1)} %copy-done.4, bf16[32,128,512]{2,1,0:T(8,128)(2,1)S(1)} %fusion.9), kind=kLoop, calls=%fused_computation.18 | loop fusion | flops 18874304 | bytes 12583168 | tf_op jit(solution)/shard_map/reduce_sum | solution.py:74
  183.9 0.6 pad_maximum_fusion.12
  (21 shorter events, 0.1 us)
Async XLA Ops:
  2.0 22.8 %all-to-all-start = ((s32[1,128,2]{2,0,1:T(1,128)}), s32[1,128,2]{2,0,1:T(1,128)S(1)}, u32[]{:S(2)}, u32[]{:S(2)}) async-start(s32[1,128,2]{2,0,1:T(1,128)} %copy.27), calls=%async_computation | async-start | bytes 131072 | tf_op jit(solution)/shard_map/all_to_all | solution.py:40
  14.2 67.6 %collective-permute-start.1 = (bf16[1,128,512]{2,1,0:T(8,128)(2,1)S(1)}, bf16[1,128,512]{2,1,0:T(8,128)(2,1)S(1)}, u32[]{:S(2)}, u32[]{:S(2)}) collective-permute-start(bf16[1,128,512]{2,1,0:T(8,128)(2,1)S(1)} %get-tuple-element.6), channel_id=1, source_target_pairs={{1,0},{2,1},{3,2},{4,3},{5,4},{6,5},{7,6},{8,7},{9,8},{10,9},{11,1... | collective-permute-start | bytes 393224 | tf_op jit(solution)/shard_map/ppermute | solution.py:18
  21.3 30.9 %collective-permute-start = (bf16[1,128,512]{2,1,0:T(8,128)(2,1)S(1)}, bf16[1,128,512]{2,1,0:T(8,128)(2,1)S(1)}, u32[]{:S(2)}, u32[]{:S(2)}) collective-permute-start(bf16[1,128,512]{2,1,0:T(8,128)(2,1)S(1)} %get-tuple-element.7), channel_id=1, source_target_pairs={{0,1},{1,2},{2,3},{3,4},{4,5},{5,6},{6,7},{7,8},{8,9},{9,10},{10,1... | collective-permute-start | bytes 393224 | tf_op jit(solution)/shard_map/ppermute | solution.py:15
  25.0 14.8 %copy-start.6 = (bf16[1,128,2,8,128]{4,3,2,1,0:T(8,128)(2,1)S(1)}, bf16[1,128,2,8,128]{4,3,2,1,0:T(8,128)(2,1)}, u32[]{:S(2)}) copy-start(bf16[1,128,2,8,128]{4,3,2,1,0:T(8,128)(2,1)} %param.13) | copy-start | bytes 1572868
  29.4 39.5 %all-to-all-start.1 = ((bf16[128,2,8,512]{3,2,1,0:T(8,128)(2,1)}), bf16[128,2,8,512]{3,2,1,0:T(8,128)(2,1)}, u32[]{:S(2)}, u32[]{:S(2)}) async-start(bf16[128,2,8,512]{3,2,1,0:T(8,128)(2,1)} %bitcast.14), calls=%async_computation.1 | async-start | bytes 4194304 | tf_op jit(solution)/shard_map/all_to_all | solution.py:25
  45.0 7.2 %copy-start.7 = (s32[4096]{0:T(1024)S(1)}, s32[4096]{0:T(1024)}, u32[]{:S(2)}) copy-start(s32[4096]{0:T(1024)} %param.8) | copy-start | bytes 49156
  45.0 7.2 %copy-start = (bf16[4096,512]{1,0:T(8,128)(2,1)S(1)}, bf16[4096,512]{1,0:T(8,128)(2,1)}, u32[]{:S(2)}) copy-start(bf16[4096,512]{1,0:T(8,128)(2,1)} %param.7) | copy-start | bytes 12582916
  68.9 12.9 %copy-start.1 = (bf16[4096,512]{1,0:T(8,128)(2,1)S(1)}, bf16[4096,512]{1,0:T(8,128)(2,1)}, u32[]{:S(2)}) copy-start(bf16[4096,512]{1,0:T(8,128)(2,1)} %param.7) | copy-start | bytes 12582916
  106.8 42.5 %all-to-all-start.2 = ((bf16[128,2,8,512]{3,2,1,0:T(8,128)(2,1)}), bf16[128,2,8,512]{3,2,1,0:T(8,128)(2,1)}, u32[]{:S(2)}, u32[]{:S(2)}) async-start(bf16[128,2,8,512]{3,2,1,0:T(8,128)(2,1)} %bitcast.82), calls=%async_computation.2 | async-start | bytes 4194304 | tf_op jit(solution)/shard_map/all_to_all | solution.py:25
  113.6 30.0 %copy-start.3 = (bf16[32,128,512]{2,1,0:T(8,128)(2,1)S(1)}, bf16[32,128,512]{2,1,0:T(8,128)(2,1)}, u32[]{:S(2)}) copy-start(bf16[32,128,512]{2,1,0:T(8,128)(2,1)} %fusion.8) | copy-start | bytes 12582916
  113.6 30.0 %collective-permute-start.2 = (bf16[1,128,512]{2,1,0:T(8,128)(2,1)S(1)}, bf16[1,128,512]{2,1,0:T(8,128)(2,1)S(1)}, u32[]{:S(2)}, u32[]{:S(2)}) collective-permute-start(bf16[1,128,512]{2,1,0:T(8,128)(2,1)S(1)} %get-tuple-element.5), channel_id=1, source_target_pairs={{0,1},{1,2},{2,3},{3,4},{4,5},{5,6},{6,7},{7,8},{8,9},{9,10},{10,1... | collective-permute-start | bytes 393224 | tf_op jit(solution)/shard_map/ppermute | solution.py:15
  120.8 41.4 %collective-permute-start.3 = (bf16[1,128,512]{2,1,0:T(8,128)(2,1)S(1)}, bf16[1,128,512]{2,1,0:T(8,128)(2,1)S(1)}, u32[]{:S(2)}, u32[]{:S(2)}) collective-permute-start(bf16[1,128,512]{2,1,0:T(8,128)(2,1)S(1)} %get-tuple-element.4), channel_id=1, source_target_pairs={{1,0},{2,1},{3,2},{4,3},{5,4},{6,5},{7,6},{8,7},{9,8},{10,9},{11,1... | collective-permute-start | bytes 393224 | tf_op jit(solution)/shard_map/ppermute | solution.py:18
  149.3 12.9 %copy-start.4 = (bf16[32,128,512]{2,1,0:T(8,128)(2,1)S(1)}, bf16[32,128,512]{2,1,0:T(8,128)(2,1)}, u32[]{:S(2)}) copy-start(bf16[32,128,512]{2,1,0:T(8,128)(2,1)} %fusion.8) | copy-start | bytes 12582916
  162.2 13.7 %copy-start.2 = (bf16[4096,512]{1,0:T(8,128)(2,1)S(1)}, bf16[4096,512]{1,0:T(8,128)(2,1)}, u32[]{:S(2)}) copy-start(bf16[4096,512]{1,0:T(8,128)(2,1)} %param.7) | copy-start | bytes 12582916
  180.9 3.1 %copy-start.5 = (bf16[32,128,512]{2,1,0:T(8,128)(2,1)}, bf16[32,128,512]{2,1,0:T(8,128)(2,1)S(1)}, u32[]{:S(2)}) copy-start(bf16[32,128,512]{2,1,0:T(8,128)(2,1)S(1)} %fusion.9) | copy-start | bytes 12582916
where the time goes:
time: 185 us
  matrix products  78.7 us (43%)
  starting transfers between devices  40.9 us (22%)
  waiting for transfers between devices  26.7 us (14%)
  other arithmetic  23.1 us (12%)
  local copies, waits for them, and re-layouts  14.3 us (8%)
    dot_general x6, matrix products, body(): jnp.einsum('itr,irc->itc', band_w[:, offset + 1], source, preferred_eleme...  52.9 us
    dot_general x2, matrix products, body(): jnp.einsum('tqr,qc->trc', placed, received.reshape(-1, classes), preferre...  25.8 us
    ppermute x2, waiting for transfers between devices, with_halo(): lax.ppermute(lax.slice_in_dim(block, block.shape[dim] - width, None, axis...  15.6 us
    all_to_all x2, starting transfers between devices, fetch_blocks(): lax.all_to_all(blocks, 'node', split_axis=0, concat_axis=0, tiled=True)  15.4 us
    ppermute x2, starting transfers between devices, with_halo(): lax.ppermute(lax.slice_in_dim(block, 0, width, axis=dim), axis, backward)  14.3 us
    convert_element_type x2, other arithmetic, body(): fresh = jnp.where(seeded, clamped, scaled).astype(jnp.bfloat16)  12.1 us
    all_to_all x1, starting transfers between devices, body(): lax.all_to_all(far_block, 'node', split_axis=1, concat_axis=0, tiled=True)  11.2 us
    all_to_all x2, waiting for transfers between devices, fetch_blocks(): lax.all_to_all(blocks, 'node', split_axis=0, concat_axis=0, tiled=True)  11 us
  transfers between devices with their start and end apart: 7, of which 2 were waited for; matrix products, arithmetic and copies ran while one was open for 37% of the time, Pallas kernels for 0%

commit v1 on v0

v1 whole, which is shorter than its diff:
```python
import functools
import itertools

import jax
import jax.numpy as jnp
import numpy as np
from jax import lax
from jax.experimental import pallas as pl
from jax.experimental.pallas import tpu as pltpu
from jax.sharding import PartitionSpec as P

MESH = pl.DeviceIdType.MESH
N = 128
TILES = 32
C = 512
F32 = jnp.float32
BF16 = jnp.bfloat16


def offset_order():
    chips = [c for c in itertools.product(range(4), repeat=3) if any(c)]
    hops = lambda c: sum(min(v, 4 - v) for v in c)
    seen, groups = set(), []
    for c in chips:
        if c in seen:
            continue
        group = set()
        for r in range(3):
            q = c[r:] + c[:r]
            group |= {q, tuple((-v) % 4 for v in q)}
        seen |= group
        groups.append(sorted(group))
    groups.sort(key=lambda g: -hops(g[0]))
    flat = [c for g in groups for c in g]
    order = [c + (1,) for c in flat] + [(0, 0, 0, 1)] + [c + (0,) for c in flat]
    return order + [(0, 0, 0, 0)]


ORDER = offset_order()
PIECES = ((0, 64), (64, 96), (96, 112), (112, 128))


def shifted(me, o):
    z = ((me >> 5) + o[0]) & 3
    x = ((me >> 3) + o[1]) & 3
    y = ((me >> 1) + o[2]) & 3
    return (z << 5) | (x << 3) | (y << 1) | ((me & 1) ^ o[3])


def back(o):
    return tuple((-v) % 4 for v in o[:3]) + (o[3],)


def kernel(
    labels, seed, band, wants, tiles, counts, far_w, code, out, res,
    lab, new, edge, bw, fw, wr, wt, tv, acc, deg, mask, ask, asked, flip, picks, send, got1, got2, rsum,
    load_sem, ask_send, ask_recv, pick_sem, send_sem, got_sem, halo_send, halo_recv,
):
    me = lax.axis_index("node")
    right, left = (me + 1) & (N - 1), (me + N - 1) & (N - 1)

    loads = [
        pltpu.make_async_copy(labels, lab, load_sem.at[0]),
        pltpu.make_async_copy(band, bw, load_sem.at[1]),
        pltpu.make_async_copy(far_w, fw, load_sem.at[2]),
    ]
    for copy in loads:
        copy.start()

    barrier = pltpu.get_barrier_semaphore()
    for o in ORDER[:-1]:
        pl.semaphore_signal(barrier, inc=1, device_id=(shifted(me, o),), device_id_type=MESH)

    flip[...] = jnp.zeros((N, N), jnp.int32)
    flip[0:2, :] = wants[...]
    ask[...] = jnp.transpose(flip[...]).reshape(N, 1, N)

    ones = jnp.ones((384, N), BF16)
    loads[0].wait()
    loads[1].wait()

    def band_lhs(t):
        return jnp.concatenate([bw[t, 0], bw[t, 1], bw[t, 2]], axis=1)

    def band_tile(cur, t):
        rows = pl.ds(pl.multiple_of(t * 128, 128), 128)
        around = cur[pl.ds(pl.multiple_of((t - 1) * 16, 16), 48)].reshape(384, C)
        acc[rows, :] = jnp.dot(band_lhs(t), around, preferred_element_type=F32)

    def band_ends(cur, sweep):
        low = jnp.concatenate([edge[2 * sweep], cur[0:32]], axis=0).reshape(384, C)
        acc[0:128, :] = jnp.dot(band_lhs(0), low, preferred_element_type=F32)
        high = jnp.concatenate([cur[TILES * 16 - 32 :], edge[2 * sweep + 1]], axis=0).reshape(384, C)
        acc[(TILES - 1) * 128 :, :] = jnp.dot(band_lhs(TILES - 1), high, preferred_element_type=F32)

    def first_band(t, carry):
        band_tile(lab, t)
        return carry

    lax.fori_loop(1, TILES - 1, first_band, 0)

    pl.semaphore_wait(barrier, N - 1)

    for j, o in enumerate(ORDER[:-1]):
        peer = shifted(me, o)
        pltpu.make_async_remote_copy(
            src_ref=ask.at[peer], dst_ref=asked.at[j], send_sem=ask_send, recv_sem=ask_recv,
            device_id=(peer,), device_id_type=MESH,
        ).start()

    def halo(cur, sweep):
        return [
            pltpu.make_async_remote_copy(
                src_ref=cur.at[pl.ds((TILES - 1) * 16, 16)], dst_ref=edge.at[2 * sweep],
                send_sem=halo_send.at[2 * sweep], recv_sem=halo_recv.at[2 * sweep],
                device_id=(right,), device_id_type=MESH,
            ),
            pltpu.make_async_remote_copy(
                src_ref=cur.at[pl.ds(0, 16)], dst_ref=edge.at[2 * sweep + 1],
                send_sem=halo_send.at[2 * sweep + 1], recv_sem=halo_recv.at[2 * sweep + 1],
                device_id=(left,), device_id_type=MESH,
            ),
        ]

    halo1 = halo(lab, 0)
    for copy in halo1:
        copy.start()
    asked[N - 1] = ask[me]

    loads[2].wait()
    for j, o in enumerate(ORDER):
        wr[16 * j : 16 * (j + 1), :] = fw[shifted(me, o)].reshape(16, N)
    for j in range(0, 2048, 128):
        wt[:, j : j + 128] = jnp.transpose(wr[j : j + 128, :].astype(F32)).astype(BF16)
    slot = lax.broadcasted_iota(jnp.int32, (2, N), 0)
    goal = jnp.where(slot < counts[...], tiles[...], 64).astype(F32).astype(BF16)
    goal = jnp.concatenate([goal, jnp.zeros((14, N), BF16)], axis=0)
    o = code[...]
    source = (
        ((((me >> 5) + (o >> 5)) & 3) << 5)
        | ((((me >> 3) + (o >> 3)) & 3) << 3)
        | ((((me >> 1) + (o >> 1)) & 3) << 1)
        | ((me ^ o) & 1)
    )
    spread = (lax.broadcasted_iota(jnp.int32, (N, 2048), 0) == source).astype(F32).astype(BF16)
    both = jnp.dot(goal, spread, preferred_element_type=F32)
    second = ((lax.broadcasted_iota(jnp.int32, (1, 2048), 1) >> 3) & 1) == 1
    tv[...] = jnp.where(second, both[1:2], both[0:1]).astype(jnp.int32)

    def far_lhs(p, j0, j1):
        w = wt[:, 16 * j0 : 16 * j1]
        to = tv[:, 16 * j0 : 16 * j1]
        parts = [w * (to == 2 * p + i).astype(F32).astype(BF16) for i in range(2)]
        return jnp.concatenate(parts, axis=0)

    def prepare(p, carry):
        rows = pl.ds(pl.multiple_of(p * 256, 256), 256)
        total = jnp.dot(far_lhs(p, 0, N), jnp.ones((2048, N), BF16), preferred_element_type=F32)
        bands = jnp.concatenate([band_lhs(2 * p), band_lhs(2 * p + 1)], axis=0)
        deg[rows, :] = 0.05 * (total + jnp.dot(bands, ones, preferred_element_type=F32))
        for i in range(2):
            row = seed[pl.ds(2 * p + i, 1), :].astype(F32)
            square = jnp.broadcast_to(row, (N, N))
            start = pl.multiple_of(p * 256 + i * 128, 128)
            mask[pl.ds(start, 128), :] = jnp.transpose(square)
        return carry

    lax.fori_loop(0, TILES // 2, prepare, 0)

    pltpu.make_async_copy(asked.at[pl.ds(0, N - 1)], asked.at[pl.ds(0, N - 1)], ask_recv).wait()
    flip[...] = jnp.transpose(asked[...].reshape(N, N))
    to_scalars = pltpu.make_async_copy(flip.at[pl.ds(0, 8)], picks, pick_sem)
    to_scalars.start()
    to_scalars.wait()

    def piece_of(j):
        return [i for i, (a, b) in enumerate(PIECES) if a <= j < b][0]

    def push(cur, got, sweep):
        def gather(lo, hi):
            def one(j, carry):
                for k in range(2):
                    send[2 * j + k] = cur[picks[k, j]]
                return carry

            lax.fori_loop(lo, hi, one, 0, unroll=4)

        def start(lo, hi):
            for j in range(lo, hi):
                pltpu.make_async_remote_copy(
                    src_ref=send.at[pl.ds(2 * j, 2)], dst_ref=got.at[pl.ds(2 * j, 2)],
                    send_sem=send_sem.at[sweep], recv_sem=got_sem.at[4 * sweep + piece_of(j)],
                    device_id=(shifted(me, back(ORDER[j])),), device_id_type=MESH,
                ).start()

        for k in range(2):
            got[2 * (N - 1) + k] = cur[picks[k, N - 1]]
        gather(0, 32)
        gather(32, 64)
        start(0, 32)
        gather(64, 96)
        start(32, 64)
        gather(96, 127)
        start(64, 127)

    def take(got, sweep, i):
        j0, j1 = PIECES[i]
        part = got.at[pl.ds(2 * j0, 2 * (min(j1, N - 1) - j0))]
        pltpu.make_async_copy(part, part, got_sem.at[4 * sweep + i]).wait()

    def far_piece(got, i, p):
        j0, j1 = PIECES[i]
        rhs = got[2 * j0 : 2 * j1].reshape(16 * (j1 - j0), C)
        return jnp.dot(far_lhs(p, j0, j1), rhs, preferred_element_type=F32)

    def sweep_far(got, sweep, finish):
        for i in range(len(PIECES) - 1):
            take(got, sweep, i)

            def add(p, carry):
                rows = pl.ds(pl.multiple_of(p * 256, 256), 256)
                acc[rows, :] = acc[rows, :] + far_piece(got, i, p)
                return carry

            lax.fori_loop(0, TILES // 2, add, 0)
        last = len(PIECES) - 1
        take(got, sweep, last)

        def end(p, carry):
            rows = pl.ds(pl.multiple_of(p * 256, 256), 256)
            x = acc[rows, :] + far_piece(got, last, p)
            square = jnp.sum(x * x, axis=1, keepdims=True)
            low = deg[rows, :]
            scale = 1.0 / jnp.maximum(jnp.sqrt(square * (1.0 / C)), low)
            scaled = x * jnp.concatenate([scale] * 4, axis=1)
            m = mask[rows, :]
            keep = jnp.concatenate([m] * 4, axis=1) == 1.0
            start = lab[pl.ds(pl.multiple_of(p * 32, 32), 32)].reshape(256, C)
            fresh = jnp.where(keep, start.astype(F32), scaled).astype(BF16)
            finish(p, fresh)
            return carry

        lax.fori_loop(0, TILES // 2, end, 0)

    def change(sweep, p, fresh, before):
        moved = jnp.abs(fresh.astype(F32) - before.astype(F32))
        for i in range(2):
            part = moved[128 * i : 128 * (i + 1)]
            lanes = part[:, 0:128] + part[:, 128:256] + part[:, 256:384] + part[:, 384:512]
            rsum[sweep * TILES + 2 * p + i] = jnp.sum(lanes.reshape(16, 8, 128), axis=0)

    push(lab, got1, 0)
    for copy in halo1:
        copy.wait()
    band_ends(lab, 0)

    def keep_new(p, fresh):
        new[pl.ds(pl.multiple_of(p * 32, 32), 32)] = fresh.reshape(32, 8, C)

    sweep_far(got1, 0, keep_new)

    sent = send.at[pl.ds(0, 2 * (N - 1))]
    pltpu.make_async_copy(sent, sent, send_sem.at[0]).wait()
    push(new, got2, 1)
    halo2 = halo(new, 1)
    for copy in halo2:
        copy.start()

    def second_band(t, carry):
        band_tile(new, t)
        return carry

    lax.fori_loop(1, TILES - 1, second_band, 0)

    def first_change(p, carry):
        block = pl.ds(pl.multiple_of(p * 32, 32), 32)
        change(0, p, new[block].reshape(256, C), lab[block].reshape(256, C))
        return carry

    lax.fori_loop(0, TILES // 2, first_change, 0)
    for copy in halo2:
        copy.wait()
    band_ends(new, 1)

    def keep_out(p, fresh):
        rows = pl.ds(pl.multiple_of(p * 256, 256), 256)
        out[rows, :] = fresh
        block = pl.ds(pl.multiple_of(p * 32, 32), 32)
        change(1, p, fresh, new[block].reshape(256, C))

    sweep_far(got2, 1, keep_out)
    res[...] = jnp.sum(jnp.sum(rsum[...], axis=1), axis=1, keepdims=True)

    pltpu.make_async_copy(sent, sent, send_sem.at[1]).wait()
    rows_sent = asked.at[pl.ds(0, N - 1)]
    pltpu.make_async_copy(rows_sent, rows_sent, ask_send).wait()


def body(labels, seed_mask, band_w, far_block, far_tile, far_count, far_w):
    code = np.array([(o[0] << 5) | (o[1] << 3) | (o[2] << 1) | o[3] for o in ORDER], np.int32)
    vmem = pl.BlockSpec(memory_space=pltpu.VMEM)
    hbm = pl.BlockSpec(memory_space=pl.ANY)
    dma = pltpu.SemaphoreType.DMA
    out, res = pl.pallas_call(
        kernel,
        out_shape=(
            jax.ShapeDtypeStruct((TILES * 128, C), BF16),
            jax.ShapeDtypeStruct((2 * TILES, 1), F32),
        ),
        in_specs=[hbm, vmem, hbm, vmem, vmem, vmem, hbm, vmem],
        out_specs=(vmem, vmem),
        scratch_shapes=[
            pltpu.VMEM((TILES * 16, 8, C), BF16),
            pltpu.VMEM((TILES * 16, 8, C), BF16),
            pltpu.VMEM((4, 16, 8, C), BF16),
            pltpu.VMEM((TILES, 3, 128, 128), BF16),
            pltpu.VMEM((N, 2, 8, 128), BF16),
            pltpu.VMEM((2048, 128), BF16),
            pltpu.VMEM((128, 2048), BF16),
            pltpu.VMEM((1, 2048), jnp.int32),
            pltpu.VMEM((TILES * 128, C), F32),
            pltpu.VMEM((TILES * 128, 128), F32),
            pltpu.VMEM((TILES * 128, 128), F32),
            pltpu.VMEM((N, 1, N), jnp.int32),
            pltpu.VMEM((N, 1, N), jnp.int32),
            pltpu.VMEM((N, N), jnp.int32),
            pltpu.SMEM((8, N), jnp.int32),
            pltpu.VMEM((2 * N, 8, C), BF16),
            pltpu.VMEM((2 * N, 8, C), BF16),
            pltpu.VMEM((2 * N, 8, C), BF16),
            pltpu.VMEM((2 * TILES, 8, 128), F32),
            dma((3,)), dma, dma, dma, dma((2,)), dma((8,)), dma((4,)), dma((4,)),
        ],
        compiler_params=pltpu.CompilerParams(
            collective_id=0, has_side_effects=True, vmem_limit_bytes=48 << 20
        ),
    )(
        labels.reshape(TILES * 16, 8, C),
        seed_mask.reshape(TILES, 128),
        band_w,
        jnp.swapaxes(far_block, 1, 2)[0],
        jnp.swapaxes(far_tile, 1, 2)[0],
        far_count,
        far_w[0],
        jnp.asarray(np.repeat(code, 16)[None]),
    )
    return out, res.reshape(2, TILES)


def solution(mesh):
    placed = (
        P("node", None),
        P("node"),
        P("node", None, None, None),
        P("node", None, None),
        P("node", None, None),
        P("node", None),
        P("node", None, None, None, None),
    )
    return jax.shard_map(
        body,
        mesh=mesh,
        in_specs=placed,
        out_specs=(P("node", None), P(None, "node")),
        check_vma=False,
    )
```

time: 185 us -> 127 us (0.69)
  Pallas kernels: 0 us -> 114 us
  matrix products: 78.7 us -> 0 us
  starting transfers between devices: 40.9 us -> 0 us
  waiting for transfers between devices: 26.7 us -> 0 us
  other arithmetic: 23.1 us -> 0.11 us
  local copies, waits for them, and re-layouts: 14.3 us -> 11.5 us
    pallas_call x0 -> x1, Pallas kernels: none -> 114 us  [body(): pl.pallas_call(kernel, out_shape=(jax.ShapeDtypeStruct((TILES * 128, C),...]
    dot_general x8 -> x0, matrix products: 78.7 us -> none  [the longest x6 52.9 us: body(): jnp.einsum('itr,irc->itc', band_w[:, offset + 1], source, preferred_eleme...]
    all_to_all x3 -> x0, starting transfers between devices: 26.6 us -> none  [the longest x2 15.4 us: fetch_blocks(): lax.all_to_all(blocks, 'node', split_axis=0, concat_axis=0, tiled=True)]
    ppermute x4 -> x0, waiting for transfers between devices: 15.7 us -> none  [the longest x2 15.6 us: with_halo(): lax.ppermute(lax.slice_in_dim(block, block.shape[dim] - width, None, axis...]
    ppermute x4 -> x0, starting transfers between devices: 14.3 us -> none  [the longest x2 14.3 us: with_halo(): lax.ppermute(lax.slice_in_dim(block, 0, width, axis=dim), axis, backward)]
    convert_element_type x2 -> x0, other arithmetic: 12.1 us -> none  [body(): fresh = jnp.where(seeded, clamped, scaled).astype(jnp.bfloat16)]
    all_to_all x3 -> x0, waiting for transfers between devices: 11 us -> none  [the longest x2 11 us: fetch_blocks(): lax.all_to_all(blocks, 'node', split_axis=0, concat_axis=0, tiled=True)]
    gather x2 -> x0, local copies, waits for them, and re-layouts: 8.59 us -> none  [fetch_blocks(): blocks = current.reshape(-1, block_rows, classes)[requests]]
  transfers between devices with their start and end apart: 7 -> 0, of which waited for: 2 -> 0; matrix products, arithmetic and copies ran while one was open for 37% -> 0% of each run, Pallas kernels for 0% -> 0%
where the time goes in v1:
time: 127 us; the launch traced here: 126 us
  Pallas kernels  114 us (90%)
  local copies, waits for them, and re-layouts  11.5 us (9%)
    pallas_call x1, Pallas kernels, body(): pl.pallas_call(kernel, out_shape=(jax.ShapeDtypeStruct((TILES * 128, C),...  114 us
    unnamed x15, local copies, waits for them, and re-layouts  10.8 us

profile of v1, /device:TPU:0, one launch (start us, length us, event | category | flops | bytes accessed | tf_op | source)
XLA Modules:
  0.0 126.5 jit_solution(2320292210658375518)
XLA Ops:
  0.6 0.0 copy-start
  0.6 1.9 %copy-done = bf16[32,3,128,128]{3,2,1,0:T(8,128)(2,1)S(1)} copy-done((bf16[32,3,128,128]{3,2,1,0:T(8,128)(2,1)S(1)}, bf16[32,3,128,128]{3,2,1,0:T(8,128)(2,1)}, u32[]{:S(2)}) %copy-start) | copy-done | bytes 3145752
  2.5 0.0 copy-start.1
  2.5 1.0 copy-done.1
  3.6 0.0 copy-start.2
  3.6 0.7 copy-done.2
  4.3 0.0 copy-start.3
  4.3 0.7 copy-done.3
  5.0 0.0 copy-start.4
  5.0 0.7 copy-done.4
  5.7 0.0 copy-start.5
  5.7 0.7 copy-done.5
  6.3 0.0 copy-start.6
  6.3 0.7 copy-done.6
  7.0 114.2 %shard_map.95 = (bf16[4096,512]{1,0:T(8,128)(2,1)}, f32[64,1]{1,0:T(8,128)S(1)}) custom-call(bf16[512,8,512]{2,1,0:T(8,128)(2,1)} %bitcast.13, s32[32,128]{1,0:T(8,128)S(1)} %bitcast.10, bf16[32,3,128,128]{3,2,1,0:T(8,128)(2,1)S(1)} %copy-done, s32[2,128]{1,0:T(2,128)S(1)} %bitcast.11, s32[2,128]{1,0:T(2,128)S(1)} %bitcast.12, s32[1,128]{1,0:T(1,128)S(1)} %copy-done.6, ...), custom_call_target="tpu_custom_call" | custom-call | tf_op jit(solution)/shard_map/pallas_call | solution.py:304
  121.2 0.1 reduce
  121.3 0.7 reshape.15
  122.0 4.5 %copy.11 = bf16[4096,512]{1,0:T(8,128)(2,1)} copy(bf16[4096,512]{1,0:T(8,128)(2,1)} %get-tuple-element.8) | data formatting | bytes 8388608
Async XLA Ops:
  0.6 1.9 %copy-start = (bf16[32,3,128,128]{3,2,1,0:T(8,128)(2,1)S(1)}, bf16[32,3,128,128]{3,2,1,0:T(8,128)(2,1)}, u32[]{:S(2)}) copy-start(bf16[32,3,128,128]{3,2,1,0:T(8,128)(2,1)} %band.1) | copy-start | bytes 9437188
  2.5 1.0 copy-start.1
  3.6 0.7 copy-start.2
  4.3 0.7 copy-start.3
  5.0 0.7 copy-start.4
  5.7 0.7 copy-start.5
  6.3 0.7 copy-start.6

commit v2 on v1

v2 whole, which is shorter than its diff:
```python
import functools
import itertools

import jax
import jax.numpy as jnp
import numpy as np
from jax import lax
from jax.experimental import pallas as pl
from jax.experimental.pallas import tpu as pltpu
from jax.sharding import PartitionSpec as P

MESH = pl.DeviceIdType.MESH
N = 128
TILES = 32
C = 512
F32 = jnp.float32
BF16 = jnp.bfloat16


GROUPS = (
    (4, 5, 37, 47, 26, 50, 63, 28),
    (17, 10, 44, 2, 9, 36, 59, 35),
    (7, 40, 33, 12, 1, 38, 42, 15),
    (3, 20, 13, 25, 46, 34, 55, 56),
    (53, 18, 24, 11, 52, 45, 62, 19),
    (60, 6, 61, 16, 31, 54, 23, 41),
    (48, 21, 14, 8, 32, 58, 30, 39),
    (51, 22, 29, 43, 57, 49, 27, 0),
)
SIZE = 16
AHEAD = 4
PASSES = ((0, 2), (2, 4), (4, 6), (6, 8))
WIDE = 4
ADD_UNROLL = 2
END_UNROLL = 2
BAND_UNROLL = 2


def offset_order():
    hops = lambda v: sum(min(d, 4 - d) for d in (v >> 4, (v >> 2) & 3, v & 3))
    order = []
    for group in GROUPS:
        for v in sorted(group, key=lambda v: -hops(v)):
            order += [(v >> 4, (v >> 2) & 3, v & 3, c) for c in (1, 0)]
    return order


ORDER = offset_order()


def shifted(me, o):
    z = ((me >> 5) + o[0]) & 3
    x = ((me >> 3) + o[1]) & 3
    y = ((me >> 1) + o[2]) & 3
    return (z << 5) | (x << 3) | (y << 1) | ((me & 1) ^ o[3])


def back(o):
    return tuple((-v) % 4 for v in o[:3]) + (o[3],)


def kernel(
    labels, seed_in, band, wants_in, tiles_in, counts_in, far_w, code_in, out, res,
    seed, wants, tiles, counts, code, lab, new, edge, bw, fw, wr, wt, tv, acc, deg, mask, ask, asked, flip, picks, send, got1, got2, rsum, far_deg,
    load_sem, ask_send, ask_recv, pick_sem, send_sem, got_sem, halo_send, halo_recv,
):
    me = lax.axis_index("node")
    right, left = (me + 1) & (N - 1), (me + N - 1) & (N - 1)

    loads = [
        pltpu.make_async_copy(wants_in, wants, load_sem.at[0]),
        pltpu.make_async_copy(labels, lab, load_sem.at[1]),
        pltpu.make_async_copy(band, bw, load_sem.at[2]),
        pltpu.make_async_copy(far_w, fw, load_sem.at[3]),
        pltpu.make_async_copy(tiles_in, tiles, load_sem.at[4]),
        pltpu.make_async_copy(counts_in, counts, load_sem.at[5]),
        pltpu.make_async_copy(seed_in, seed, load_sem.at[6]),
        pltpu.make_async_copy(code_in, code, load_sem.at[7]),
    ]
    for copy in loads:
        copy.start()

    barrier = pltpu.get_barrier_semaphore()
    for o in ORDER[:-1]:
        pl.semaphore_signal(barrier, inc=1, device_id=(shifted(me, o),), device_id_type=MESH)

    loads[0].wait()
    flip[...] = jnp.zeros((N, N), jnp.int32)
    flip[0:2, :] = wants[...]
    ask[...] = jnp.transpose(flip[...]).reshape(N, 1, N)

    ones = jnp.ones((384, N), BF16)

    def band_lhs(t):
        return jnp.concatenate([bw[t, 0], bw[t, 1], bw[t, 2]], axis=1)

    def band_tile(cur, t):
        rows = pl.ds(pl.multiple_of(t * 128, 128), 128)
        around = cur[pl.ds(pl.multiple_of((t - 1) * 16, 16), 48)].reshape(384, C)
        acc[rows, :] = jnp.dot(band_lhs(t), around, preferred_element_type=F32)

    def band_ends(cur):
        low = jnp.concatenate([bw[0, 1], bw[0, 2]], axis=1)
        acc[0:128, :] = jnp.dot(low, cur[0:32].reshape(256, C), preferred_element_type=F32)
        high = jnp.concatenate([bw[TILES - 1, 0], bw[TILES - 1, 1]], axis=1)
        around = cur[TILES * 16 - 32 :].reshape(256, C)
        acc[(TILES - 1) * 128 :, :] = jnp.dot(high, around, preferred_element_type=F32)

    def add_edges(halos, sweep):
        for copy in halos:
            copy.wait()
        for rows, w, side in ((slice(0, 128), bw[0, 0], 0), (slice(TILES * 128 - 128, None), bw[TILES - 1, 2], 1)):
            part = edge[2 * sweep + side].reshape(128, C)
            acc[rows, :] = acc[rows, :] + jnp.dot(w, part, preferred_element_type=F32)

    def first_band(t, carry):
        band_tile(lab, t)
        return carry

    pl.semaphore_wait(barrier, N - 1)

    for j, o in enumerate(ORDER[:-1]):
        peer = shifted(me, o)
        pltpu.make_async_remote_copy(
            src_ref=ask.at[peer], dst_ref=asked.at[j], send_sem=ask_send, recv_sem=ask_recv,
            device_id=(peer,), device_id_type=MESH,
        ).start()

    def halo(cur, sweep):
        return [
            pltpu.make_async_remote_copy(
                src_ref=cur.at[pl.ds((TILES - 1) * 16, 16)], dst_ref=edge.at[2 * sweep],
                send_sem=halo_send.at[2 * sweep], recv_sem=halo_recv.at[2 * sweep],
                device_id=(right,), device_id_type=MESH,
            ),
            pltpu.make_async_remote_copy(
                src_ref=cur.at[pl.ds(0, 16)], dst_ref=edge.at[2 * sweep + 1],
                send_sem=halo_send.at[2 * sweep + 1], recv_sem=halo_recv.at[2 * sweep + 1],
                device_id=(left,), device_id_type=MESH,
            ),
        ]

    loads[1].wait()
    halo1 = halo(lab, 0)
    for copy in halo1:
        copy.start()
    asked[N - 1] = ask[me]

    for copy in loads[2:]:
        copy.wait()
    for j, o in enumerate(ORDER):
        wr[16 * j : 16 * (j + 1), :] = fw[shifted(me, o)].reshape(16, N)
    for j in range(0, 2048, 128):
        wt[:, j : j + 128] = jnp.transpose(wr[j : j + 128, :].astype(F32)).astype(BF16)
    slot = lax.broadcasted_iota(jnp.int32, (2, N), 0)
    goal = jnp.where(slot < counts[...], tiles[...], 64).astype(F32).astype(BF16)
    goal = jnp.concatenate([goal, jnp.zeros((14, N), BF16)], axis=0)
    o = code[...]
    source = (
        ((((me >> 5) + (o >> 5)) & 3) << 5)
        | ((((me >> 3) + (o >> 3)) & 3) << 3)
        | ((((me >> 1) + (o >> 1)) & 3) << 1)
        | ((me ^ o) & 1)
    )
    spread = (lax.broadcasted_iota(jnp.int32, (N, 2304), 0) == source).astype(F32).astype(BF16)
    both = jnp.dot(goal, spread, preferred_element_type=F32)
    lane = lax.broadcasted_iota(jnp.int32, (1, 2304), 1)
    second = jnp.where(lane < 2048, lane >> 3, lane) & 1 == 1
    tv[...] = jnp.where(second, both[1:2], both[0:1]).astype(jnp.int32)

    def far_lhs(p, j0, j1, parts):
        w = wt[:, 16 * j0 : 16 * j1]
        to = tv[:, 16 * j0 : 16 * j1]
        return jnp.concatenate([w * (to == parts * p + i).astype(F32).astype(BF16) for i in range(parts)], axis=0)

    def prepare(t, carry):
        rows = pl.ds(pl.multiple_of(t * 128, 128), 128)
        bands = jnp.dot(band_lhs(t), ones, preferred_element_type=F32)
        far = jnp.transpose(jnp.broadcast_to(far_deg[pl.ds(t, 1), :], (N, N)))
        deg[rows, :] = 0.05 * (bands + far)
        mask[rows, :] = jnp.transpose(jnp.broadcast_to(seed[pl.ds(t, 1), :].astype(F32), (N, N)))
        return carry

    def prepare_all():
        slot_sums = jnp.sum(wr[...].reshape(2 * N, 8, N).astype(F32), axis=1)
        tile = lax.broadcasted_iota(jnp.int32, (TILES, 2 * N), 0)
        hit = (tv[:, 2048:2304] == tile).astype(F32)
        far_deg[...] = jnp.dot(hit, slot_sums, precision=lax.Precision.HIGHEST, preferred_element_type=F32)
        lax.fori_loop(0, TILES, prepare, 0, unroll=2)

    pltpu.make_async_copy(asked.at[pl.ds(0, N - 1)], asked.at[pl.ds(0, N - 1)], ask_recv).wait()
    flip[...] = jnp.transpose(asked[...].reshape(N, N))
    to_scalars = pltpu.make_async_copy(flip.at[pl.ds(0, 8)], picks, pick_sem)
    to_scalars.start()
    to_scalars.wait()

    def gather(cur, got, g):
        def one(j, carry):
            for k in range(2):
                send[2 * j + k] = cur[picks[k, j]]
            return carry

        last = g == len(GROUPS) - 1
        lax.fori_loop(g * SIZE, (g + 1) * SIZE - last, one, 0, unroll=4)
        if last:
            for k in range(2):
                got[2 * (N - 1) + k] = cur[picks[k, N - 1]]

    def start(got, sweep, g):
        for j in range(g * SIZE, min((g + 1) * SIZE, N - 1)):
            pltpu.make_async_remote_copy(
                src_ref=send.at[pl.ds(2 * j, 2)], dst_ref=got.at[pl.ds(2 * j, 2)],
                send_sem=send_sem.at[sweep], recv_sem=got_sem.at[8 * sweep + g],
                device_id=(shifted(me, back(ORDER[j])),), device_id_type=MESH,
            ).start()

    def push(cur, got, sweep):
        gather(cur, got, 0)
        for g in range(1, 8):
            gather(cur, got, g)
            if g <= AHEAD:
                start(got, sweep, g - 1)

    def take(got, sweep, g):
        part = got.at[pl.ds(2 * g * SIZE, 2 * (min((g + 1) * SIZE, N - 1) - g * SIZE))]
        pltpu.make_async_copy(part, part, got_sem.at[8 * sweep + g]).wait()
        if g + AHEAD < 8:
            start(got, sweep, g + AHEAD)

    def far_piece(got, g0, g1, p, parts):
        rhs = got[2 * SIZE * g0 : 2 * SIZE * g1].reshape(16 * SIZE * (g1 - g0), C)
        return jnp.dot(far_lhs(p, g0 * SIZE, g1 * SIZE, parts), rhs, preferred_element_type=F32)

    def far_add(got, g0, g1):
        def add(p, carry):
            rows = pl.ds(pl.multiple_of(p * 128 * WIDE, 128 * WIDE), 128 * WIDE)
            acc[rows, :] = acc[rows, :] + far_piece(got, g0, g1, p, WIDE)
            return carry

        lax.fori_loop(0, TILES // WIDE, add, 0, unroll=ADD_UNROLL)

    def sweep_far(got, sweep, finish, between):
        for g0, g1 in PASSES[:-1]:
            for g in range(g0, g1):
                take(got, sweep, g)
            far_add(got, g0, g1)
            if g1 in between:
                between[g1]()
        last = PASSES[-1]
        for g in range(*last):
            take(got, sweep, g)

        def end(p, carry):
            rows = pl.ds(pl.multiple_of(p * 256, 256), 256)
            x = acc[rows, :] + far_piece(got, *last, p, 2)
            square = jnp.sum(x * x, axis=1, keepdims=True)
            low = deg[rows, :]
            scale = 1.0 / jnp.maximum(jnp.sqrt(square * (1.0 / C)), low)
            scaled = x * jnp.concatenate([scale] * 4, axis=1)
            m = mask[rows, :]
            keep = jnp.concatenate([m] * 4, axis=1) == 1.0
            given = lab[pl.ds(pl.multiple_of(p * 32, 32), 32)].reshape(256, C)
            fresh = jnp.where(keep, given.astype(F32), scaled).astype(BF16)
            finish(p, fresh)
            return carry

        lax.fori_loop(0, TILES // 2, end, 0, unroll=END_UNROLL)

    def change(sweep, p, fresh, before):
        moved = jnp.abs(fresh.astype(F32) - before.astype(F32))
        for i in range(2):
            part = moved[128 * i : 128 * (i + 1)]
            lanes = part[:, 0:128] + part[:, 128:256] + part[:, 256:384] + part[:, 384:512]
            rsum[sweep * TILES + 2 * p + i] = jnp.sum(lanes.reshape(16, 8, 128), axis=0)

    push(lab, got1, 0)
    band_ends(lab)
    lax.fori_loop(1, TILES - 1, first_band, 0, unroll=BAND_UNROLL)

    def while_arriving_1():
        prepare_all()
        add_edges(halo1, 0)

    def keep_new(p, fresh):
        new[pl.ds(pl.multiple_of(p * 32, 32), 32)] = fresh.reshape(32, 8, C)

    sweep_far(got1, 0, keep_new, {4: while_arriving_1})

    sent = send.at[pl.ds(0, 2 * (N - 1))]
    pltpu.make_async_copy(sent, sent, send_sem.at[0]).wait()
    halo2 = halo(new, 1)
    for copy in halo2:
        copy.start()
    push(new, got2, 1)
    band_ends(new)

    def second_band(t, carry):
        band_tile(new, t)
        return carry

    lax.fori_loop(1, TILES - 1, second_band, 0, unroll=BAND_UNROLL)

    def first_change(p, carry):
        block = pl.ds(pl.multiple_of(p * 32, 32), 32)
        change(0, p, new[block].reshape(256, C), lab[block].reshape(256, C))
        return carry

    def while_arriving_2():
        lax.fori_loop(0, TILES // 2, first_change, 0)
        add_edges(halo2, 1)

    def keep_out(p, fresh):
        rows = pl.ds(pl.multiple_of(p * 256, 256), 256)
        out[rows, :] = fresh
        block = pl.ds(pl.multiple_of(p * 32, 32), 32)
        change(1, p, fresh, new[block].reshape(256, C))

    sweep_far(got2, 1, keep_out, {4: while_arriving_2})
    sums = jnp.concatenate([jnp.sum(rsum[...], axis=1), jnp.zeros((64, N), F32)], axis=0)
    row = jnp.sum(jnp.transpose(sums), axis=0, keepdims=True)
    res[0:1, :] = row[:, 0:TILES]
    res[1:2, :] = row[:, TILES : 2 * TILES]

    pltpu.make_async_copy(sent, sent, send_sem.at[1]).wait()
    rows_sent = asked.at[pl.ds(0, N - 1)]
    pltpu.make_async_copy(rows_sent, rows_sent, ask_send).wait()


def body(labels, seed_mask, band_w, far_block, far_tile, far_count, far_w):
    code = np.array([(o[0] << 5) | (o[1] << 3) | (o[2] << 1) | o[3] for o in ORDER], np.int32)
    vmem = pl.BlockSpec(memory_space=pltpu.VMEM)
    hbm = pl.BlockSpec(memory_space=pltpu.HBM)
    dma = pltpu.SemaphoreType.DMA
    out, res = pl.pallas_call(
        kernel,
        out_shape=(
            pltpu.VMEM((TILES * 128, C), BF16),
            pltpu.VMEM((2, TILES), F32),
        ),
        in_specs=[hbm] * 8,
        out_specs=(vmem, vmem),
        scratch_shapes=[
            pltpu.VMEM((TILES, 128), jnp.int32),
            pltpu.VMEM((2, N), jnp.int32),
            pltpu.VMEM((2, N), jnp.int32),
            pltpu.VMEM((1, N), jnp.int32),
            pltpu.VMEM((1, 2304), jnp.int32),
            pltpu.VMEM((TILES * 16, 8, C), BF16),
            pltpu.VMEM((TILES * 16, 8, C), BF16),
            pltpu.VMEM((4, 16, 8, C), BF16),
            pltpu.VMEM((TILES, 3, 128, 128), BF16),
            pltpu.VMEM((N, 2, 8, 128), BF16),
            pltpu.VMEM((2048, 128), BF16),
            pltpu.VMEM((128, 2048), BF16),
            pltpu.VMEM((1, 2304), jnp.int32),
            pltpu.VMEM((TILES * 128, C), F32),
            pltpu.VMEM((TILES * 128, 128), F32),
            pltpu.VMEM((TILES * 128, 128), F32),
            pltpu.VMEM((N, 1, N), jnp.int32),
            pltpu.VMEM((N, 1, N), jnp.int32),
            pltpu.VMEM((N, N), jnp.int32),
            pltpu.SMEM((8, N), jnp.int32),
            pltpu.VMEM((2 * N, 8, C), BF16),
            pltpu.VMEM((2 * N, 8, C), BF16),
            pltpu.VMEM((2 * N, 8, C), BF16),
            pltpu.VMEM((2 * TILES, 8, 128), F32),
            pltpu.VMEM((TILES, 128), F32),
            dma((8,)), dma, dma, dma, dma((2,)), dma((16,)), dma((4,)), dma((4,)),
        ],
        compiler_params=pltpu.CompilerParams(
            collective_id=0, has_side_effects=True, vmem_limit_bytes=48 << 20
        ),
    )(*[
        pltpu.with_memory_space_constraint(x, pltpu.HBM)
        for x in (
            labels.reshape(TILES * 16, 8, C),
            seed_mask.reshape(TILES, 128),
            band_w,
            jnp.swapaxes(far_block, 1, 2)[0],
            jnp.swapaxes(far_tile, 1, 2)[0],
            far_count,
            far_w[0],
            jnp.asarray(np.concatenate([np.repeat(code, 16), np.repeat(code, 2)])[None]),
        )
    ])
    return out, res


def solution(mesh):
    placed = (
        P("node", None),
        P("node"),
        P("node", None, None, None),
        P("node", None, None),
        P("node", None, None),
        P("node", None),
        P("node", None, None, None, None),
    )
    return jax.shard_map(
        body,
        mesh=mesh,
        in_specs=placed,
        out_specs=(P("node", None), P(None, "node")),
        check_vma=False,
    )
```

time: 127 us -> 96.9 us (0.76)
  Pallas kernels: 114 us -> 93.1 us
  local copies, waits for them, and re-layouts: 11.5 us -> 2.58 us
    pallas_call x1, Pallas kernels: 114 us -> 93.1 us  [body(): pl.pallas_call(kernel, out_shape=(pltpu.VMEM((TILES * 128, C), BF16), plt...]
    unnamed x15 -> x2, local copies, waits for them, and re-layouts: 10.8 us -> 2.58 us
where the time goes in v2:
time: 96.9 us; the launch traced here: 96.4 us
  Pallas kernels  93.1 us (96%)
  local copies, waits for them, and re-layouts  2.58 us (3%)
    pallas_call x1, Pallas kernels, body(): pl.pallas_call(kernel, out_shape=(pltpu.VMEM((TILES * 128, C), BF16), plt...  93.1 us
    unnamed x2, local copies, waits for them, and re-layouts  2.58 us

profile of v2, /device:TPU:0, one launch (start us, length us, event | category | flops | bytes accessed | tf_op | source)
XLA Modules:
  0.0 96.4 jit_solution(11302461339100178845)
XLA Ops:
  0.6 93.1 %shard_map.95 = (bf16[4096,512]{1,0:T(8,128)(2,1)S(1)}, f32[2,32]{1,0:T(2,128)S(1)}) custom-call(bf16[512,8,512]{2,1,0:T(8,128)(2,1)} %bitcast.9, s32[32,128]{1,0:T(8,128)} %bitcast.11, bf16[32,3,128,128]{3,2,1,0:T(8,128)(2,1)} %band.1, s32[2,128]{1,0:T(2,128)} %bitcast.12, s32[2,128]{1,0:T(2,128)} %bitcast.13, s32[1,128]{1,0:T(1,128)} %counts_in.1, ...), custom_call_target="tpu_custom_call" | custom-call | tf_op jit(solution)/shard_map/pallas_call | solution.py:334
  93.8 2.0 %copy.12 = bf16[4096,512]{1,0:T(8,128)(2,1)} copy(bf16[4096,512]{1,0:T(8,128)(2,1)S(1)} %get-tuple-element.2) | data formatting | bytes 8388608
  95.8 0.6 copy.13

commit v3 on v2

--- a/solution.py
+++ b/solution.py
@@ -28,11 +28,11 @@
     (51, 22, 29, 43, 57, 49, 27, 0),
 )
 SIZE = 16
-AHEAD = 4
+AHEAD = (6, 6)
 PASSES = ((0, 2), (2, 4), (4, 6), (6, 8))
 WIDE = 4
 ADD_UNROLL = 2
-END_UNROLL = 2
+END_UNROLL = 4
 BAND_UNROLL = 2
 
 
@@ -216,16 +216,17 @@
 
     def push(cur, got, sweep):
         gather(cur, got, 0)
-        for g in range(1, 8):
-            gather(cur, got, g)
-            if g <= AHEAD:
+        for g in range(1, 9):
+            if g < 8:
+                gather(cur, got, g)
+            if g <= AHEAD[sweep]:
                 start(got, sweep, g - 1)
 
     def take(got, sweep, g):
         part = got.at[pl.ds(2 * g * SIZE, 2 * (min((g + 1) * SIZE, N - 1) - g * SIZE))]
         pltpu.make_async_copy(part, part, got_sem.at[8 * sweep + g]).wait()
-        if g + AHEAD < 8:
-            start(got, sweep, g + AHEAD)
+        if g + AHEAD[sweep] < 8:
+            start(got, sweep, g + AHEAD[sweep])
 
     def far_piece(got, g0, g1, p, parts):
         rhs = got[2 * SIZE * g0 : 2 * SIZE * g1].reshape(16 * SIZE * (g1 - g0), C)
@@ -289,9 +290,9 @@
     sent = send.at[pl.ds(0, 2 * (N - 1))]
     pltpu.make_async_copy(sent, sent, send_sem.at[0]).wait()
     halo2 = halo(new, 1)
+    push(new, got2, 1)
     for copy in halo2:
         copy.start()
-    push(new, got2, 1)
     band_ends(new)
 
     def second_band(t, carry):

time: 96.9 us -> 92.2 us (0.951)
  the two profiles are of different devices: /device:TPU:0 before, /device:TPU:12 now
where the time goes in v3:
time: 92.2 us; the launch traced here: 92.1 us
  Pallas kernels  88.9 us (96%)
  local copies, waits for them, and re-layouts  2.58 us (3%)
    pallas_call x1, Pallas kernels, body(): pl.pallas_call(kernel, out_shape=(pltpu.VMEM((TILES * 128, C), BF16), plt...  88.9 us
    unnamed x2, local copies, waits for them, and re-layouts  2.58 us

profile of v3, /device:TPU:12, one launch (start us, length us, event | category | flops | bytes accessed | tf_op | source)
XLA Modules:
  0.0 92.1 jit_solution(8465761419081358494)
XLA Ops:
  0.6 88.9 %shard_map.95 = (bf16[4096,512]{1,0:T(8,128)(2,1)S(1)}, f32[2,32]{1,0:T(2,128)S(1)}) custom-call(bf16[512,8,512]{2,1,0:T(8,128)(2,1)} %bitcast.9, s32[32,128]{1,0:T(8,128)} %bitcast.11, bf16[32,3,128,128]{3,2,1,0:T(8,128)(2,1)} %band.1, s32[2,128]{1,0:T(2,128)} %bitcast.12, s32[2,128]{1,0:T(2,128)} %bitcast.13, s32[1,128]{1,0:T(1,128)} %counts_in.1, ...), custom_call_target="tpu_custom_call" | custom-call | tf_op jit(solution)/shard_map/pallas_call | solution.py:335
  89.5 2.0 %copy.12 = bf16[4096,512]{1,0:T(8,128)(2,1)} copy(bf16[4096,512]{1,0:T(8,128)(2,1)S(1)} %get-tuple-element.2) | data formatting | bytes 8388608
  91.5 0.6 copy.13

commit v4 on v3

--- a/solution.py
+++ b/solution.py
@@ -29,7 +29,7 @@
 )
 SIZE = 16
 AHEAD = (6, 6)
-PASSES = ((0, 2), (2, 4), (4, 6), (6, 8))
+PASSES = ((0, 3), (3, 6), (6, 8))
 WIDE = 4
 ADD_UNROLL = 2
 END_UNROLL = 4
@@ -278,14 +278,15 @@
     band_ends(lab)
     lax.fori_loop(1, TILES - 1, first_band, 0, unroll=BAND_UNROLL)
 
+    prepare_all()
+
     def while_arriving_1():
-        prepare_all()
         add_edges(halo1, 0)
 
     def keep_new(p, fresh):
         new[pl.ds(pl.multiple_of(p * 32, 32), 32)] = fresh.reshape(32, 8, C)
 
-    sweep_far(got1, 0, keep_new, {4: while_arriving_1})
+    sweep_far(got1, 0, keep_new, {3: while_arriving_1})
 
     sent = send.at[pl.ds(0, 2 * (N - 1))]
     pltpu.make_async_copy(sent, sent, send_sem.at[0]).wait()
@@ -306,8 +307,9 @@
         change(0, p, new[block].reshape(256, C), lab[block].reshape(256, C))
         return carry
 
+    lax.fori_loop(0, TILES // 2, first_change, 0)
+
     def while_arriving_2():
-        lax.fori_loop(0, TILES // 2, first_change, 0)
         add_edges(halo2, 1)
 
     def keep_out(p, fresh):
@@ -316,7 +318,7 @@
         block = pl.ds(pl.multiple_of(p * 32, 32), 32)
         change(1, p, fresh, new[block].reshape(256, C))
 
-    sweep_far(got2, 1, keep_out, {4: while_arriving_2})
+    sweep_far(got2, 1, keep_out, {3: while_arriving_2})
     sums = jnp.concatenate([jnp.sum(rsum[...], axis=1), jnp.zeros((64, N), F32)], axis=0)
     row = jnp.sum(jnp.transpose(sums), axis=0, keepdims=True)
     res[0:1, :] = row[:, 0:TILES]

time: 92.2 us -> 89.6 us (0.972)
  the two profiles are of different devices: /device:TPU:12 before, /device:TPU:0 now
where the time goes in v4:
time: 89.6 us; the launch traced here: 89.1 us
  Pallas kernels  85.9 us (96%)
  local copies, waits for them, and re-layouts  2.58 us (3%)
    pallas_call x1, Pallas kernels, body(): pl.pallas_call(kernel, out_shape=(pltpu.VMEM((TILES * 128, C), BF16), plt...  85.9 us
    unnamed x2, local copies, waits for them, and re-layouts  2.58 us

profile of v4, /device:TPU:0, one launch (start us, length us, event | category | flops | bytes accessed | tf_op | source)
XLA Modules:
  0.0 89.1 jit_solution(12878123357614226222)
XLA Ops:
  0.6 85.9 %shard_map.95 = (bf16[4096,512]{1,0:T(8,128)(2,1)S(1)}, f32[2,32]{1,0:T(2,128)S(1)}) custom-call(bf16[512,8,512]{2,1,0:T(8,128)(2,1)} %bitcast.9, s32[32,128]{1,0:T(8,128)} %bitcast.11, bf16[32,3,128,128]{3,2,1,0:T(8,128)(2,1)} %band.1, s32[2,128]{1,0:T(2,128)} %bitcast.12, s32[2,128]{1,0:T(2,128)} %bitcast.13, s32[1,128]{1,0:T(1,128)} %counts_in.1, ...), custom_call_target="tpu_custom_call" | custom-call | tf_op jit(solution)/shard_map/pallas_call | solution.py:337
  86.6 2.0 %copy.12 = bf16[4096,512]{1,0:T(8,128)(2,1)} copy(bf16[4096,512]{1,0:T(8,128)(2,1)S(1)} %get-tuple-element.2) | data formatting | bytes 8388608
  88.6 0.6 copy.13
